TPU v7x, 32 devices: a whole 2x2x4 slice. The times are simulated.
32 devices in a mesh: seg: 8 (over z, core), tok: 4 (over y, x).
Axes of the slice: x: 2, y: 2, z: 4, core: 2. Of those that a mesh axis runs over, the one named last changes fastest.
Arguments:
- queries: bfloat16 [2, 8, 2, 5120, 256], P(None, 'seg', None, 'tok'), may hold values from -6 to 6
- key_vectors: bfloat16 [2, 8, 2, 5120, 256], P(None, 'seg', None, 'tok'), may hold values from -6 to 6
- values: bfloat16 [2, 8, 2, 5120, 256], P(None, 'seg', None, 'tok'), may hold values from -6 to 6
- token_rates: float32 [2, 8, 2, 5120], P(None, 'seg', None, 'tok'), may hold values from 0.05 to 3
- fast_weights: float32 [8, 3, 256, 256], P('seg', None, None, 'tok'), may hold values from -0.375 to 0.375
- momenta: float32 [8, 3, 256, 256], P('seg', None, None, 'tok'), may hold values from -3 to 3
- fresh_weights: float32 [3, 256, 256], P(None, None, 'tok'), may hold values from -0.375 to 0.375
- fresh_momenta: float32 [3, 256, 256], P(None, None, 'tok'), may hold values from -3 to 3
Outputs:
- outputs: bfloat16 [2, 8, 2, 5120, 256], P(None, 'seg', None, 'tok')
- final_weights: float32 [8, 3, 256, 256], P('seg', None, None, 'tok')
- final_momenta: float32 [8, 3, 256, 256], P('seg', None, None, 'tok')
All inputs are finite; a program needn't handle non-finite values.
Results may differ from a plain program's by a relative error of at most 0.033.
Values may be sent and summed in bfloat16 or wider, within the bound.
A program may use at most 64 MiB of HBM per device.

v0:
```python
import jax
import jax.numpy as jnp
from jax import lax
from jax.sharding import PartitionSpec as P

momentum_decay = 0.9
learn_rate = 0.05
epsilon = 1e-06


def shifted(array, axis, by):
    length = lax.axis_size(axis)
    pairs = [(i, i + by) for i in range(length) if 0 <= i + by < length]
    return lax.ppermute(array, axis, pairs)


def silu_parts(pre_gate):
    sigmoid_gate = jax.nn.sigmoid(pre_gate)
    return (pre_gate * sigmoid_gate, sigmoid_gate * (1.0 + pre_gate * (1.0 - sigmoid_gate)))


def local_grads(usable_weights, key_rows, value_rows, rate_rows):
    pre_gate = jnp.dot(key_rows, usable_weights[0], preferred_element_type=jnp.float32)
    pre_up = jnp.dot(key_rows, usable_weights[2], preferred_element_type=jnp.float32)
    active, slope_gate = silu_parts(pre_gate)
    hidden = (active * pre_up).astype(jnp.bfloat16)
    scaled = (rate_rows[:, None] * value_rows.astype(jnp.float32)).astype(jnp.bfloat16)
    back_hidden = -lax.dot_general(
        scaled, usable_weights[1], (((1,), (1,)), ((), ())), preferred_element_type=jnp.float32
    )
    back_gate = (back_hidden * pre_up * slope_gate).astype(jnp.bfloat16)
    back_up = (back_hidden * active).astype(jnp.bfloat16)
    contract_rows = (((0,), (0,)), ((), ()))
    grad_gate = lax.dot_general(
        key_rows, back_gate, contract_rows, preferred_element_type=jnp.float32
    )
    grad_down = -lax.dot_general(hidden, scaled, contract_rows, preferred_element_type=jnp.float32)
    grad_up = lax.dot_general(key_rows, back_up, contract_rows, preferred_element_type=jnp.float32)
    return (jnp.stack([grad_gate, grad_down, grad_up]), jnp.sum(rate_rows * rate_rows))


def update(weights, moment, gradients, rate_total):
    moment = momentum_decay * moment + gradients * lax.rsqrt(rate_total)
    stepped = weights - learn_rate * moment
    rescale = jnp.sqrt(
        jnp.sum(weights * weights, axis=1, keepdims=True)
        / (jnp.sum(stepped * stepped, axis=1, keepdims=True) + epsilon)
    )
    return (stepped * rescale, moment)


def apply_fast(usable_weights, query_rows):
    pre_gate = jnp.dot(query_rows, usable_weights[0], preferred_element_type=jnp.float32)
    pre_up = jnp.dot(query_rows, usable_weights[2], preferred_element_type=jnp.float32)
    hidden = (jax.nn.silu(pre_gate) * pre_up).astype(jnp.bfloat16)
    return jnp.dot(hidden, usable_weights[1], preferred_element_type=jnp.float32).astype(
        jnp.bfloat16
    )


def usable(weights):
    rounded = weights.astype(jnp.bfloat16)
    return lax.all_gather(rounded, "tok", axis=2, tiled=True)


def advance(weights, moment, usable_weights, query_rows, key_rows, value_rows, rate_rows):
    gradients, square = local_grads(usable_weights, key_rows, value_rows, rate_rows)
    gradients = lax.psum_scatter(
        gradients.astype(jnp.bfloat16), "tok", scatter_dimension=2, tiled=True
    ).astype(jnp.float32)
    summed = lax.psum(square, "tok")
    weights, moment = update(weights, moment, gradients, summed)
    usable_weights = usable(weights)
    return (weights, moment, usable_weights, apply_fast(usable_weights, query_rows))


def body(
    queries, key_vectors, values, token_rates, fast_weights, momenta, fresh_weights, fresh_momenta
):
    sections = queries.shape[0]
    blocks = queries.shape[2]
    weights, moment, fresh_start, fresh_moment = (
        fast_weights[0],
        momenta[0],
        fresh_weights,
        fresh_momenta,
    )
    is_first = lax.axis_index("seg") == 0
    results = []
    for wave_step in range(sections):
        if wave_step > 0:
            passed = (
                shifted(weights.astype(jnp.bfloat16), "seg", 1).astype(weights.dtype),
                shifted(moment.astype(jnp.bfloat16), "seg", 1).astype(moment.dtype),
            )
            weights = jnp.where(is_first, fresh_start, passed[0])
            moment = jnp.where(is_first, fresh_moment, passed[1])
        usable_weights = usable(weights)
        for block_index in range(blocks):
            weights, moment, usable_weights, result = advance(
                weights,
                moment,
                usable_weights,
                queries[wave_step, 0, block_index],
                key_vectors[wave_step, 0, block_index],
                values[wave_step, 0, block_index],
                token_rates[wave_step, 0, block_index],
            )
            results.append(result)
    row_count = queries.shape[3]
    head_width = queries.shape[4]
    outputs = jnp.stack(results).reshape(sections, blocks, row_count, head_width)[:, None]
    return (outputs, weights[None], moment[None])


def solution(mesh):
    return jax.shard_map(
        body,
        mesh=mesh,
        in_specs=(
            P(None, "seg", None, "tok", None),
            P(None, "seg", None, "tok", None),
            P(None, "seg", None, "tok", None),
            P(None, "seg", None, "tok"),
            P("seg", None, None, "tok"),
            P("seg", None, None, "tok"),
            P(None, None, "tok"),
            P(None, None, "tok"),
        ),
        out_specs=(
            P(None, "seg", None, "tok", None),
            P("seg", None, None, "tok"),
            P("seg", None, None, "tok"),
        ),
        check_vma=False,
    )
```

profile of v0, /device:TPU:0, one launch (start us, length us, event | category | flops | bytes accessed | tf_op | source)
XLA Modules:
  0.0 212.2 jit_solution(14321896189256100010)
XLA Ops:
  8.3 11.0 %all_gather.18 = bf16[3,256,256]{1,2,0:T(8,128)(2,1)S(1)} all-gather(bf16[3,256,64]{1,2,0:T(8,128)(2,1)S(1)} %bitcast_convert_fusion), channel_id=1, replica_groups=mesh['seg'=8,'tok'=4] {'tok'}, dimensions={2}, use_global_device_ids=true | all-gather | bytes 491520 | tf_op jit(solution)/shard_map/all_gather | solution.py:63
  23.7 1.9 fusion.43
  28.5 9.6 %all-reduce = (f32[]{:T(128)}, f32[]{:T(128)}, f32[]{:T(128)}, f32[]{:T(128)}) all-reduce(f32[]{:T(128)} %get-tuple-element.34, f32[]{:T(128)} %get-tuple-element.33, f32[]{:T(128)} %get-tuple-element.32, f32[]{:T(128)} %get-tuple-element.31), channel_id=1, replica_groups=mesh['seg'=8,'tok'=4] {'tok'}, use_global_device_ids=true, to_apply=%region_2.0 | all-reduce | flops 4 | bytes 32 | tf_op jit(solution)/shard_map/psum | solution.py:71
  38.8 13.5 %reduce-scatter.5.cloned.1.call-done = bf16[3,256,64]{1,2,0:T(8,128)(2,1)} async-done(((bf16[3,256,256]{1,2,0:T(8,128)(2,1)}), bf16[3,256,64]{1,2,0:T(8,128)(2,1)}) %reduce-scatter.5.cloned.1.call-update) | async-done | bytes 98320 | tf_op jit(solution)/shard_map/reduce_scatter | solution.py:68
  53.5 9.9 %all_gather.19 = bf16[3,256,256]{1,2,0:T(8,128)(2,1)S(1)} all-gather(bf16[3,256,64]{1,2,0:T(8,128)(2,1)S(1)} %multiply_convert_fusion.27), channel_id=1, replica_groups=mesh['seg'=8,'tok'=4] {'tok'}, dimensions={2}, use_global_device_ids=true | all-gather | bytes 491520 | tf_op jit(solution)/shard_map/all_gather | solution.py:63
  66.2 1.9 fusion.42
  70.4 24.1 %reduce-scatter.7.cloned.1.call-done = bf16[3,256,64]{1,2,0:T(8,128)(2,1)} async-done(((bf16[3,256,256]{1,2,0:T(8,128)(2,1)}), bf16[3,256,64]{1,2,0:T(8,128)(2,1)}) %reduce-scatter.7.cloned.1.call-update) | async-done | bytes 98320 | tf_op jit(solution)/shard_map/reduce_scatter | solution.py:68
  94.5 1.7 multiply_reduce_fusion.4
  99.1 10.0 %all_gather.21 = bf16[3,256,256]{1,2,0:T(8,128)(2,1)S(1)} all-gather(bf16[3,256,64]{1,2,0:T(8,128)(2,1)S(1)} %fusion.145), channel_id=1, replica_groups=mesh['seg'=8,'tok'=4] {'tok'}, dimensions={2}, use_global_device_ids=true | all-gather | bytes 491520 | tf_op jit(solution)/shard_map/all_gather | solution.py:63
  111.9 1.9 fusion.41
  115.5 2.5 %convolution_bitcast_fusion.13 = f32[1280,256]{1,0:T(8,128)} fusion(bf16[2,1,2,1280,256]{4,3,2,1,0:T(8,128)(2,1)} %param.8, bf16[3,256,256]{1,2,0:T(8,128)(2,1)S(1)} %all_gather.19), kind=kOutput, calls=%fused_computation.20 | convolution fusion | flops 167772160 | bytes 2097152 | tf_op jit(solution)/shard_map/dot_general | solution.py:53
  118.0 3.0 %fusion.8 = bf16[1,1280,256]{2,1,0:T(8,128)(2,1)} fusion(f32[1280,256]{1,0:T(8,128)} %convolution_bitcast_fusion.13, bf16[2,1,2,1280,256]{4,3,2,1,0:T(8,128)(2,1)} %param.8, bf16[3,256,256]{1,2,0:T(8,128)(2,1)S(1)} %all_gather.19), kind=kOutput, calls=%fused_computation.31 | convolution fusion | flops 337838080 | bytes 2883584 | tf_op jit(solution)/shard_map/dot_general | solution.py:56
  121.0 2.3 %collective-permute-start.1 = (bf16[3,256,64]{1,2,0:T(8,128)(2,1)}, bf16[3,256,64]{1,2,0:T(8,128)(2,1)S(1)}, u32[]{:S(2)}, u32[]{:S(2)}) collective-permute-start(bf16[3,256,64]{1,2,0:T(8,128)(2,1)} %get-tuple-element.23), channel_id=1, source_target_pairs={{0,4},{4,8},{8,12},{12,16},{16,20},{20,24},{24,28},{1,5},{5,9},{9,... | collective-permute-start | bytes 294920 | tf_op jit(solution)/shard_map/ppermute | solution.py:14
  123.3 10.1 %all_gather.20 = bf16[3,256,256]{1,2,0:T(8,128)(2,1)S(1)} all-gather(bf16[3,256,64]{1,2,0:T(8,128)(2,1)S(1)} %multiply_convert_fusion.24), channel_id=1, replica_groups=mesh['seg'=8,'tok'=4] {'tok'}, dimensions={2}, use_global_device_ids=true | all-gather | bytes 491520 | tf_op jit(solution)/shard_map/all_gather | solution.py:63
  133.3 2.7 %convolution_bitcast_fusion.9 = f32[1280,256]{1,0:T(8,128)} fusion(bf16[2,1,2,1280,256]{4,3,2,1,0:T(8,128)(2,1)} %param.8, bf16[3,256,256]{1,2,0:T(8,128)(2,1)S(1)} %all_gather.20), kind=kOutput, calls=%fused_computation.14 | convolution fusion | flops 167772160 | bytes 2097152 | tf_op jit(solution)/shard_map/dot_general | solution.py:53
  136.0 7.1 %reduce-scatter.9.cloned.1.call-done = bf16[3,256,64]{1,2,0:T(8,128)(2,1)} async-done(((bf16[3,256,256]{1,2,0:T(8,128)(2,1)}), bf16[3,256,64]{1,2,0:T(8,128)(2,1)}) %reduce-scatter.9.cloned.1.call-update) | async-done | bytes 98320 | tf_op jit(solution)/shard_map/reduce_scatter | solution.py:68
  144.4 10.2 %all_gather.22 = bf16[3,256,256]{1,2,0:T(8,128)(2,1)S(1)} all-gather(bf16[3,256,64]{1,2,0:T(8,128)(2,1)S(1)} %multiply_convert_fusion.26), channel_id=1, replica_groups=mesh['seg'=8,'tok'=4] {'tok'}, dimensions={2}, use_global_device_ids=true | all-gather | bytes 491520 | tf_op jit(solution)/shard_map/all_gather | solution.py:63
  157.4 1.9 fusion.40
  160.9 3.2 %fusion.9 = bf16[1,1280,256]{2,1,0:T(8,128)(2,1)} fusion(f32[1280,256]{1,0:T(8,128)} %convolution_bitcast_fusion.9, bf16[2,1,2,1280,256]{4,3,2,1,0:T(8,128)(2,1)} %param.8, bf16[3,256,256]{1,2,0:T(8,128)(2,1)} %copy-done.5), kind=kOutput, calls=%fused_computation.32 | convolution fusion | flops 337838080 | bytes 2883584 | tf_op jit(solution)/shard_map/dot_general | solution.py:56
  165.5 2.8 %fusion.10 = bf16[1,1280,256]{2,1,0:T(8,128)(2,1)} fusion(f32[1280,256]{1,0:T(8,128)} %convolution_bitcast_fusion.5, bf16[2,1,2,1280,256]{4,3,2,1,0:T(8,128)(2,1)S(1)} %copy-done.1, bf16[3,256,256]{1,2,0:T(8,128)(2,1)S(1)} %all_gather.22), kind=kOutput, calls=%fused_computation.33 | convolution fusion | flops 337838080 | bytes 2883584 | tf_op jit(solution)/shard_map/dot_general | solution.py:56
  168.3 17.3 %reduce-scatter.11.cloned.1.call-done = bf16[3,256,64]{1,2,0:T(8,128)(2,1)} async-done(((bf16[3,256,256]{1,2,0:T(8,128)(2,1)}), bf16[3,256,64]{1,2,0:T(8,128)(2,1)}) %reduce-scatter.11.cloned.1.call-update) | async-done | bytes 98320 | tf_op jit(solution)/shard_map/reduce_scatter | solution.py:68
  188.1 9.9 %all_gather.23 = bf16[3,256,256]{1,2,0:T(8,128)(2,1)S(1)} all-gather(bf16[3,256,64]{1,2,0:T(8,128)(2,1)S(1)} %get-tuple-element.29), channel_id=1, replica_groups=mesh['seg'=8,'tok'=4] {'tok'}, dimensions={2}, use_global_device_ids=true | all-gather | bytes 491520 | tf_op jit(solution)/shard_map/all_gather | solution.py:63
  199.4 2.8 %fusion.11 = bf16[1,1280,256]{2,1,0:T(8,128)(2,1)} fusion(f32[1280,256]{1,0:T(8,128)} %convolution_bitcast_fusion.1, bf16[2,1,2,1280,256]{4,3,2,1,0:T(8,128)(2,1)S(1)} %copy-done.1, bf16[3,256,256]{1,2,0:T(8,128)(2,1)S(1)} %all_gather.23), kind=kOutput, calls=%fused_computation.34 | convolution fusion | flops 337838080 | bytes 2883584 | tf_op jit(solution)/shard_map/dot_general | solution.py:56
  202.2 3.5 %pad_maximum_fusion = bf16[4,1280,256]{2,1,0:T(8,128)(2,1)} fusion(bf16[1,1280,256]{2,1,0:T(8,128)(2,1)} %fusion.11, bf16[1,1280,256]{2,1,0:T(8,128)(2,1)} %fusion.10, bf16[1,1280,256]{2,1,0:T(8,128)(2,1)} %fusion.9, bf16[1,1280,256]{2,1,0:T(8,128)(2,1)} %fusion.8), kind=kLoop, calls=%fused_computation.22 | loop fusion | flops 3932160 | bytes 5242880 | tf_op jit(solution)/shard_map/stack | solution.py:112
  (69 shorter events, 30.7 us)
Async XLA Ops:
  7.2 45.1 %reduce-scatter.5.cloned.1.call-start = ((), (), s32[]{:S(2)}) async-start(), calls=%async_computation.4 | async-start | bytes 491520 | tf_op jit(solution)/shard_map/reduce_scatter | solution.py:68
  7.2 13.5 %copy-start = (bf16[2,1,2,1280,256]{4,3,2,1,0:T(8,128)(2,1)S(1)}, bf16[2,1,2,1280,256]{4,3,2,1,0:T(8,128)(2,1)}, u32[]{:S(2)}) copy-start(bf16[2,1,2,1280,256]{4,3,2,1,0:T(8,128)(2,1)} %param.9) | copy-start | bytes 7864324
  20.8 0.7 copy-start.7
  26.3 26.0 %copy-start.3 = (f32[1,3,256,64]{2,3,1,0:T(8,128)S(1)}, f32[1,3,256,64]{2,3,1,0:T(8,128)}, u32[]{:S(2)}) copy-start(f32[1,3,256,64]{2,3,1,0:T(8,128)} %param.12) | copy-start | bytes 589828
  26.3 26.0 %copy-start.4 = (f32[1,3,256,64]{2,3,1,0:T(8,128)S(1)}, f32[1,3,256,64]{2,3,1,0:T(8,128)}, u32[]{:S(2)}) copy-start(f32[1,3,256,64]{2,3,1,0:T(8,128)} %param.13) | copy-start | bytes 589828
  27.1 67.4 %reduce-scatter.7.cloned.1.call-start = ((), (), s32[]{:S(2)}) async-start(), calls=%async_computation.5 | async-start | bytes 491520 | tf_op jit(solution)/shard_map/reduce_scatter | solution.py:68
  68.1 26.4 %copy-start.6 = (bf16[3,256,64]{1,2,0:T(8,128)(2,1)S(1)}, bf16[3,256,64]{1,2,0:T(8,128)(2,1)}, u32[]{:S(2)}) copy-start(bf16[3,256,64]{1,2,0:T(8,128)(2,1)} %reduce-scatter.5.cloned.1.call-done) | copy-start | bytes 294916
  68.9 30.2 %copy-start.2 = (f32[3,256,64]{1,2,0:T(8,128)S(1)}, f32[3,256,64]{1,2,0:T(8,128)}, u32[]{:S(2)}) copy-start(f32[3,256,64]{1,2,0:T(8,128)} %param.14) | copy-start | bytes 589828
  69.7 73.4 %reduce-scatter.9.cloned.1.call-start = ((), (), s32[]{:S(2)}) async-start(), calls=%async_computation.6 | async-start | bytes 491520 | tf_op jit(solution)/shard_map/reduce_scatter | solution.py:68
  96.4 2.6 %collective-permute-start = (bf16[3,256,64]{1,2,0:T(8,128)(2,1)S(1)}, bf16[3,256,64]{1,2,0:T(8,128)(2,1)S(1)}, u32[]{:S(2)}, u32[]{:S(2)}) collective-permute-start(bf16[3,256,64]{1,2,0:T(8,128)(2,1)S(1)} %multiply_convert_fusion.24), channel_id=1, source_target_pairs={{0,4},{4,8},{8,12},{12,16},{16,20},{20,24},{24,28},{1,5},{5,9},{9,... | collective-permute-start | bytes 294920 | tf_op jit(solution)/shard_map/ppermute | solution.py:14
  115.4 70.2 %reduce-scatter.11.cloned.1.call-start = ((), (), s32[]{:S(2)}) async-start(), calls=%async_computation.7 | async-start | bytes 491520 | tf_op jit(solution)/shard_map/reduce_scatter | solution.py:68
  121.0 15.0 %collective-permute-start.1 = (bf16[3,256,64]{1,2,0:T(8,128)(2,1)}, bf16[3,256,64]{1,2,0:T(8,128)(2,1)S(1)}, u32[]{:S(2)}, u32[]{:S(2)}) collective-permute-start(bf16[3,256,64]{1,2,0:T(8,128)(2,1)} %get-tuple-element.23), channel_id=1, source_target_pairs={{0,4},{4,8},{8,12},{12,16},{16,20},{20,24},{24,28},{1,5},{5,9},{9,... | collective-permute-start | bytes 294920 | tf_op jit(solution)/shard_map/ppermute | solution.py:14
  133.3 2.7 %copy-start.5 = (bf16[3,256,256]{1,2,0:T(8,128)(2,1)}, bf16[3,256,256]{1,2,0:T(8,128)(2,1)S(1)}, u32[]{:S(2)}) copy-start(bf16[3,256,256]{1,2,0:T(8,128)(2,1)S(1)} %all_gather.20) | copy-start | bytes 1179652
  160.9 3.2 %copy-start.1 = (bf16[2,1,2,1280,256]{4,3,2,1,0:T(8,128)(2,1)S(1)}, bf16[2,1,2,1280,256]{4,3,2,1,0:T(8,128)(2,1)}, u32[]{:S(2)}) copy-start(bf16[2,1,2,1280,256]{4,3,2,1,0:T(8,128)(2,1)} %param.8) | copy-start | bytes 7864324
Sparse Core Ops, SparseCore 0:
  27.3 24.9 reduce-scatter.4
  69.8 24.6 reduce-scatter.6
  115.5 27.5 reduce-scatter.8
  161.0 24.5 reduce-scatter.10
where the time goes:
time: 213 us; the launch traced here: 212 us
  blocking collectives  70.7 us (33%)
  waiting for transfers between devices  62 us (29%)
  matrix products  42.7 us (20%)
  between operations  16.8 us (8%)
  other arithmetic  15.8 us (7%)
  starting transfers between devices  3.74 us (2%)
    reduce_scatter x4, waiting for transfers between devices, advance(): lax.psum_scatter(gradients.astype(jnp.bfloat16), 'tok', scatter_dimension...  61.9 us
    all_gather x6, blocking collectives, usable(): return lax.all_gather(rounded, 'tok', axis=2, tiled=True)  61.1 us
    dot_general x4, matrix products, apply_fast(): jnp.dot(hidden, usable_weights[1], preferred_element_type=jnp.float32)  11.8 us
    psum x1, blocking collectives, advance(): summed = lax.psum(square, 'tok')  9.65 us
    dot_general x4, matrix products, apply_fast(): jnp.dot(query_rows, usable_weights[0], preferred_element_type=jnp.float32)  8 us
    dot_general x4, matrix products, local_grads(): lax.dot_general(hidden, scaled, contract_rows, preferred_element_type=jnp...  7.57 us
    dot_general x4, matrix products, local_grads(): lax.dot_general(scaled, usable_weights[1], (((1,), (1,)), ((), ())), pref...  5.9 us
    reduce_sum x4, other arithmetic, update(): jnp.sum(stepped * stepped, axis=1, keepdims=True) + epsilon  5.57 us
  transfers between devices with their start and end apart: 6, of which 4 were waited for; matrix products, arithmetic and copies ran while one was open for 8% of the time, Pallas kernels for 0%

commit v1 on v0

--- a/solution.py
+++ b/solution.py
@@ -60,7 +60,7 @@
 
 def usable(weights):
     rounded = weights.astype(jnp.bfloat16)
-    return lax.all_gather(rounded, "tok", axis=2, tiled=True)
+    return jnp.concatenate(lax.all_gather(rounded, "tok"), axis=2)
 
 
 def advance(weights, moment, usable_weights, query_rows, key_rows, value_rows, rate_rows):

time: 213 us -> 210 us (0.986)
  matrix products: 42.7 us -> 38.5 us
  local copies, waits for them, and re-layouts: 0.45 us -> 2.7 us
    dot_general x4, matrix products: 7.57 us -> 5.38 us  [local_grads(): lax.dot_general(hidden, scaled, contract_rows, preferred_element_type=jnp...]
    dot_general x4, matrix products: 5.9 us -> 3.72 us  [local_grads(): lax.dot_general(scaled, usable_weights[1], (((1,), (1,)), ((), ())), pref...]
where the time goes in v1:
time: 210 us; the launch traced here: 209 us
  blocking collectives  71.7 us (34%)
  waiting for transfers between devices  60.1 us (29%)
  matrix products  38.5 us (18%)
  between operations  16.8 us (8%)
  other arithmetic  15.5 us (7%)
  starting transfers between devices  3.49 us (2%)
  local copies, waits for them, and re-layouts  2.7 us (1%)
    all_gather x6, blocking collectives, usable(): return jnp.concatenate(lax.all_gather(rounded, 'tok'), axis=2)  62 us
    reduce_scatter x4, waiting for transfers between devices, advance(): lax.psum_scatter(gradients.astype(jnp.bfloat16), 'tok', scatter_dimension...  60 us
    dot_general x4, matrix products, apply_fast(): jnp.dot(hidden, usable_weights[1], preferred_element_type=jnp.float32)  11.9 us
    psum x1, blocking collectives, advance(): summed = lax.psum(square, 'tok')  9.66 us
    dot_general x4, matrix products, apply_fast(): jnp.dot(query_rows, usable_weights[0], preferred_element_type=jnp.float32)  8 us
    reduce_sum x4, other arithmetic, update(): jnp.sum(stepped * stepped, axis=1, keepdims=True) + epsilon  5.65 us
    dot_general x4, matrix products, local_grads(): lax.dot_general(hidden, scaled, contract_rows, preferred_element_type=jnp...  5.38 us
  transfers between devices with their start and end apart: 6, of which 4 were waited for; matrix products, arithmetic and copies ran while one was open for 8% of the time, Pallas kernels for 0%

profile of v1, /device:TPU:0, one launch (start us, length us, event | category | flops | bytes accessed | tf_op | source)
XLA Modules:
  0.0 208.8 jit_solution(4460492597925444642)
XLA Ops:
  9.0 11.0 %all_gather.34 = bf16[4,3,256,64]{2,3,1,0:T(8,128)(2,1)S(1)} all-gather(bf16[1,3,256,64]{2,3,1,0:T(8,128)(2,1)S(1)} %convert_element_type.176), channel_id=1, replica_groups=mesh['seg'=8,'tok'=4] {'tok'}, dimensions={0}, use_global_device_ids=true | all-gather | bytes 491520 | tf_op jit(solution)/shard_map/all_gather | solution.py:63
  20.0 1.6 fusion.82
  24.4 1.9 fusion.43
  29.2 9.7 %all-reduce = (f32[]{:T(128)}, f32[]{:T(128)}, f32[]{:T(128)}, f32[]{:T(128)}) all-reduce(f32[]{:T(128)} %get-tuple-element.55, f32[]{:T(128)} %get-tuple-element.54, f32[]{:T(128)} %get-tuple-element.53, f32[]{:T(128)} %get-tuple-element.52), channel_id=1, replica_groups=mesh['seg'=8,'tok'=4] {'tok'}, use_global_device_ids=true, to_apply=%region_2.0 | all-reduce | flops 4 | bytes 32 | tf_op jit(solution)/shard_map/psum | solution.py:71
  39.6 13.5 %reduce-scatter.5.cloned.1.call-done = bf16[3,256,64]{1,2,0:T(8,128)(2,1)} async-done(((bf16[3,256,256]{1,2,0:T(8,128)(2,1)}), bf16[3,256,64]{1,2,0:T(8,128)(2,1)}) %reduce-scatter.5.cloned.1.call-update) | async-done | bytes 98320 | tf_op jit(solution)/shard_map/reduce_scatter | solution.py:68
  54.2 9.9 %all-gather = bf16[12,256,64]{1,2,0:T(8,128)(2,1)S(1)} all-gather(bf16[3,256,64]{1,2,0:T(8,128)(2,1)S(1)} %multiply_convert_fusion.27), channel_id=2, replica_groups=mesh['seg'=8,'tok'=4] {'tok'}, dimensions={0}, use_global_device_ids=true | all-gather | bytes 491520 | tf_op jit(solution)/shard_map/all_gather | solution.py:63
  67.0 1.9 fusion.42
  72.5 22.9 %reduce-scatter.7.cloned.1.call-done = bf16[3,256,64]{1,2,0:T(8,128)(2,1)} async-done(((bf16[3,256,256]{1,2,0:T(8,128)(2,1)}), bf16[3,256,64]{1,2,0:T(8,128)(2,1)}) %reduce-scatter.7.cloned.1.call-update) | async-done | bytes 98320 | tf_op jit(solution)/shard_map/reduce_scatter | solution.py:68
  95.4 1.7 multiply_reduce_fusion.4
  98.5 2.7 %convolution_bitcast_fusion.13 = f32[1280,256]{1,0:T(8,128)} fusion(bf16[256,256]{0,1:T(8,128)(2,1)S(1)} %bitcast.289, bf16[2,1,2,1280,256]{4,3,2,1,0:T(8,128)(2,1)} %param.8), kind=kOutput, calls=%fused_computation.20 | convolution fusion | flops 167772160 | bytes 2097152 | tf_op jit(solution)/shard_map/dot_general | solution.py:53
  101.2 10.3 %all-gather.2 = bf16[12,256,64]{1,2,0:T(8,128)(2,1)S(1)} all-gather(bf16[3,256,64]{1,2,0:T(8,128)(2,1)S(1)} %fusion.145), channel_id=4, replica_groups=mesh['seg'=8,'tok'=4] {'tok'}, dimensions={0}, use_global_device_ids=true | all-gather | bytes 491520 | tf_op jit(solution)/shard_map/all_gather | solution.py:63
  115.7 3.0 %fusion.8 = bf16[1,1280,256]{2,1,0:T(8,128)(2,1)} fusion(bf16[256,256]{0,1:T(8,128)(2,1)S(1)} %bitcast.295, bf16[256,256]{0,1:T(8,128)(2,1)S(1)} %bitcast.293, f32[1280,256]{1,0:T(8,128)} %convolution_bitcast_fusion.13, bf16[2,1,2,1280,256]{4,3,2,1,0:T(8,128)(2,1)} %param.8), kind=kOutput, calls=%fused_computation.31 | convolution fusion | flops 337838080 | bytes 2883584 | tf_op jit(solution)/shard_map/dot_general | solution.py:56
  118.7 2.0 collective-permute-start.1
  120.7 10.8 %all-gather.1 = bf16[12,256,64]{1,2,0:T(8,128)(2,1)S(1)} all-gather(bf16[3,256,64]{1,2,0:T(8,128)(2,1)S(1)} %multiply_convert_fusion.24), channel_id=3, replica_groups=mesh['seg'=8,'tok'=4] {'tok'}, dimensions={0}, use_global_device_ids=true | all-gather | bytes 491520 | tf_op jit(solution)/shard_map/all_gather | solution.py:63
  132.2 2.5 %convolution_bitcast_fusion.9 = f32[1280,256]{1,0:T(8,128)} fusion(bf16[256,256]{0,1:T(8,128)(2,1)S(1)} %bitcast.306, bf16[2,1,2,1280,256]{4,3,2,1,0:T(8,128)(2,1)} %param.8), kind=kOutput, calls=%fused_computation.14 | convolution fusion | flops 167772160 | bytes 2097152 | tf_op jit(solution)/shard_map/dot_general | solution.py:53
  135.4 6.3 %reduce-scatter.9.cloned.1.call-done = bf16[3,256,64]{1,2,0:T(8,128)(2,1)} async-done(((bf16[3,256,256]{1,2,0:T(8,128)(2,1)}), bf16[3,256,64]{1,2,0:T(8,128)(2,1)}) %reduce-scatter.9.cloned.1.call-update) | async-done | bytes 98320 | tf_op jit(solution)/shard_map/reduce_scatter | solution.py:68
  143.1 10.1 %all-gather.3 = bf16[12,256,64]{1,2,0:T(8,128)(2,1)S(1)} all-gather(bf16[3,256,64]{1,2,0:T(8,128)(2,1)S(1)} %multiply_convert_fusion.26), channel_id=5, replica_groups=mesh['seg'=8,'tok'=4] {'tok'}, dimensions={0}, use_global_device_ids=true | all-gather | bytes 491520 | tf_op jit(solution)/shard_map/all_gather | solution.py:63
  157.5 3.2 %fusion.9 = bf16[1,1280,256]{2,1,0:T(8,128)(2,1)} fusion(bf16[256,256]{0,1:T(8,128)(2,1)} %bitcast.308, bf16[256,256]{0,1:T(8,128)(2,1)} %bitcast.309, f32[1280,256]{1,0:T(8,128)} %convolution_bitcast_fusion.9, bf16[2,1,2,1280,256]{4,3,2,1,0:T(8,128)(2,1)} %param.8), kind=kOutput, calls=%fused_computation.32 | convolution fusion | flops 337838080 | bytes 2883584 | tf_op jit(solution)/shard_map/dot_general | solution.py:56
  162.1 2.8 %fusion.10 = bf16[1,1280,256]{2,1,0:T(8,128)(2,1)} fusion(bf16[256,256]{0,1:T(8,128)(2,1)S(1)} %bitcast.299, bf16[256,256]{0,1:T(8,128)(2,1)S(1)} %bitcast.297, f32[1280,256]{1,0:T(8,128)} %convolution_bitcast_fusion.5, bf16[2,1,2,1280,256]{4,3,2,1,0:T(8,128)(2,1)S(1)} %copy-done.3), kind=kOutput, calls=%fused_computation.33 | convolution fusion | flops 337838080 | bytes 2883584 | tf_op jit(solution)/shard_map/dot_general | solution.py:56
  164.9 17.4 %reduce-scatter.11.cloned.1.call-done = bf16[3,256,64]{1,2,0:T(8,128)(2,1)} async-done(((bf16[3,256,256]{1,2,0:T(8,128)(2,1)}), bf16[3,256,64]{1,2,0:T(8,128)(2,1)}) %reduce-scatter.11.cloned.1.call-update) | async-done | bytes 98320 | tf_op jit(solution)/shard_map/reduce_scatter | solution.py:68
  182.3 1.7 multiply_reduce_fusion
  184.7 9.9 %all-gather.4 = bf16[12,256,64]{1,2,0:T(8,128)(2,1)S(1)} all-gather(bf16[3,256,64]{1,2,0:T(8,128)(2,1)S(1)} %get-tuple-element.50), channel_id=6, replica_groups=mesh['seg'=8,'tok'=4] {'tok'}, dimensions={0}, use_global_device_ids=true | all-gather | bytes 491520 | tf_op jit(solution)/shard_map/all_gather | solution.py:63
  196.1 2.9 %fusion.11 = bf16[1,1280,256]{2,1,0:T(8,128)(2,1)} fusion(bf16[256,256]{0,1:T(8,128)(2,1)S(1)} %bitcast.310, bf16[256,256]{0,1:T(8,128)(2,1)S(1)} %bitcast.311, f32[1280,256]{1,0:T(8,128)} %convolution_bitcast_fusion.1, bf16[2,1,2,1280,256]{4,3,2,1,0:T(8,128)(2,1)S(1)} %copy-done.3), kind=kOutput, calls=%fused_computation.34 | convolution fusion | flops 337838080 | bytes 2883584 | tf_op jit(solution)/shard_map/dot_general | solution.py:56
  199.0 3.3 %pad_maximum_fusion = bf16[4,1280,256]{2,1,0:T(8,128)(2,1)} fusion(bf16[1,1280,256]{2,1,0:T(8,128)(2,1)} %fusion.11, bf16[1,1280,256]{2,1,0:T(8,128)(2,1)} %fusion.10, bf16[1,1280,256]{2,1,0:T(8,128)(2,1)} %fusion.9, bf16[1,1280,256]{2,1,0:T(8,128)(2,1)S(1)} %copy-done.7), kind=kLoop, calls=%fused_computation.22 | loop fusion | flops 3932160 | bytes 5242880 | tf_op jit(solution)/shard_map/stack | solution.py:112
  (83 shorter events, 29.2 us)
Async XLA Ops:
  7.2 45.9 %reduce-scatter.5.cloned.1.call-start = ((), (), s32[]{:S(2)}) async-start(), calls=%async_computation.4 | async-start | bytes 491520 | tf_op jit(solution)/shard_map/reduce_scatter | solution.py:68
  20.0 1.9 copy-start
  27.0 26.0 %copy-start.5 = (f32[1,3,256,64]{2,3,1,0:T(8,128)S(1)}, f32[1,3,256,64]{2,3,1,0:T(8,128)}, u32[]{:S(2)}) copy-start(f32[1,3,256,64]{2,3,1,0:T(8,128)} %param.12) | copy-start | bytes 589828
  27.0 26.0 %copy-start.6 = (f32[1,3,256,64]{2,3,1,0:T(8,128)S(1)}, f32[1,3,256,64]{2,3,1,0:T(8,128)}, u32[]{:S(2)}) copy-start(f32[1,3,256,64]{2,3,1,0:T(8,128)} %param.13) | copy-start | bytes 589828
  27.9 67.5 %reduce-scatter.7.cloned.1.call-start = ((), (), s32[]{:S(2)}) async-start(), calls=%async_computation.5 | async-start | bytes 491520 | tf_op jit(solution)/shard_map/reduce_scatter | solution.py:68
  70.4 71.3 %reduce-scatter.9.cloned.1.call-start = ((), (), s32[]{:S(2)}) async-start(), calls=%async_computation.6 | async-start | bytes 491520 | tf_op jit(solution)/shard_map/reduce_scatter | solution.py:68
  97.0 4.1 %copy-start.4 = (f32[3,256,64]{1,2,0:T(8,128)S(1)}, f32[3,256,64]{1,2,0:T(8,128)}, u32[]{:S(2)}) copy-start(f32[3,256,64]{1,2,0:T(8,128)} %param.14) | copy-start | bytes 589828
  97.2 4.0 %collective-permute-start = (bf16[3,256,64]{1,2,0:T(8,128)(2,1)S(1)}, bf16[3,256,64]{1,2,0:T(8,128)(2,1)S(1)}, u32[]{:S(2)}, u32[]{:S(2)}) collective-permute-start(bf16[3,256,64]{1,2,0:T(8,128)(2,1)S(1)} %multiply_convert_fusion.24), channel_id=1, source_target_pairs={{0,4},{4,8},{8,12},{12,16},{16,20},{20,24},{24,28},{1,5},{5,9},{9,... | collective-permute-start | bytes 294920 | tf_op jit(solution)/shard_map/ppermute | solution.py:14
  98.5 13.0 %copy-start.1 = (bf16[2,1,2,1280,256]{4,3,2,1,0:T(8,128)(2,1)S(1)}, bf16[2,1,2,1280,256]{4,3,2,1,0:T(8,128)(2,1)}, u32[]{:S(2)}) copy-start(bf16[2,1,2,1280,256]{4,3,2,1,0:T(8,128)(2,1)} %param.10) | copy-start | bytes 7864324
  101.1 10.3 %copy-start.8 = (bf16[3,256,64]{1,2,0:T(8,128)(2,1)}, bf16[3,256,64]{1,2,0:T(8,128)(2,1)S(1)}, u32[]{:S(2)}) copy-start(bf16[3,256,64]{1,2,0:T(8,128)(2,1)S(1)} %collective-permute-done) | copy-start | bytes 294916
  115.6 66.6 %reduce-scatter.11.cloned.1.call-start = ((), (), s32[]{:S(2)}) async-start(), calls=%async_computation.7 | async-start | bytes 491520 | tf_op jit(solution)/shard_map/reduce_scatter | solution.py:68
  118.7 16.1 %collective-permute-start.1 = (bf16[3,256,64]{1,2,0:T(8,128)(2,1)}, bf16[3,256,64]{1,2,0:T(8,128)(2,1)S(1)}, u32[]{:S(2)}, u32[]{:S(2)}) collective-permute-start(bf16[3,256,64]{1,2,0:T(8,128)(2,1)} %get-tuple-element.35), channel_id=1, source_target_pairs={{0,4},{4,8},{8,12},{12,16},{16,20},{20,24},{24,28},{1,5},{5,9},{9,... | collective-permute-start | bytes 294920 | tf_op jit(solution)/shard_map/ppermute | solution.py:14
  131.5 10.2 %copy-start.9 = (bf16[3,256,64]{1,2,0:T(8,128)(2,1)S(1)}, bf16[3,256,64]{1,2,0:T(8,128)(2,1)}, u32[]{:S(2)}) copy-start(bf16[3,256,64]{1,2,0:T(8,128)(2,1)} %copy-done.8) | copy-start | bytes 294916
  131.5 10.2 %copy-start.10 = (f32[3,256,64]{1,2,0:T(8,128)S(1)}, f32[3,256,64]{1,2,0:T(8,128)}, u32[]{:S(2)}) copy-start(f32[3,256,64]{1,2,0:T(8,128)} %param.15) | copy-start | bytes 589828
  134.8 0.6 copy-start.11
  141.8 11.5 %copy-start.2 = (bf16[2,1,2,1280,256]{4,3,2,1,0:T(8,128)(2,1)S(1)}, bf16[2,1,2,1280,256]{4,3,2,1,0:T(8,128)(2,1)}, u32[]{:S(2)}) copy-start(bf16[2,1,2,1280,256]{4,3,2,1,0:T(8,128)(2,1)} %param.10) | copy-start | bytes 7864324
  157.5 3.2 %copy-start.3 = (bf16[2,1,2,1280,256]{4,3,2,1,0:T(8,128)(2,1)S(1)}, bf16[2,1,2,1280,256]{4,3,2,1,0:T(8,128)(2,1)}, u32[]{:S(2)}) copy-start(bf16[2,1,2,1280,256]{4,3,2,1,0:T(8,128)(2,1)} %param.8) | copy-start | bytes 7864324
  196.1 2.9 %copy-start.7 = (bf16[1,1280,256]{2,1,0:T(8,128)(2,1)S(1)}, bf16[1,1280,256]{2,1,0:T(8,128)(2,1)}, u32[]{:S(2)}) copy-start(bf16[1,1280,256]{2,1,0:T(8,128)(2,1)} %fusion.8) | copy-start | bytes 1966084
Sparse Core Ops, SparseCore 0:
  28.0 24.9 reduce-scatter.4
  70.6 24.7 reduce-scatter.6
  115.8 25.9 reduce-scatter.8
  157.6 24.6 reduce-scatter.10
